TPU v7x, 32 devices: a whole 2x2x4 slice. The times are simulated.
32 devices in a mesh: section: 1, ep: 32 (over z, y, x, core).
Axes of the slice: x: 2, y: 2, z: 4, core: 2. Of those that a mesh axis runs over, the one named last changes fastest.
Arguments:
- saved_inputs: bfloat16 [1, 4096, 4096], P('section', 'ep'), may hold values from -6 to 6
- expert_ids: int32 [1, 4096, 2], P('section', 'ep'), may hold values from 0 to 7, as said below
- gate_weights: float32 [1, 4096, 2], P('section', 'ep'), may hold values from 0.1 to 0.9
- out_grad: bfloat16 [4096, 4096], P('ep', 'section'), may hold values from -6 to 6
- gate_w: bfloat16 [1, 7168, 4096], P('section', 'ep'), may hold values from -0.09375 to 0.09375
- up_w: bfloat16 [1, 7168, 4096], P('section', 'ep'), may hold values from -0.09375 to 0.09375
- down_w: bfloat16 [1, 7168, 4096], P('section', 'ep'), may hold values from -0.0625 to 0.0625
Outputs:
- input_grads: bfloat16 [1, 4096, 4096], P('section', 'ep')
- grad_gate: bfloat16 [1, 7168, 4096], P('section', 'ep')
- grad_up: bfloat16 [1, 7168, 4096], P('section', 'ep')
- grad_down: bfloat16 [1, 7168, 4096], P('section', 'ep')
Inputs may be any that keep to these rules, and one draw needn't show every extreme that they name: `expert_ids`: the two ids of a token differ. Among the 128 tokens of one device in one layer, at most 4 name expert 0, and in every layer some device's tokens name it exactly 4 times.
All inputs are finite; a program needn't handle non-finite values.
Results may differ from a plain program's by a relative error of at most 0.0058.
Values may be sent and summed in bfloat16 or wider, within the bound.
A program may use at most 128 MiB of HBM per device.

v0:
```python
import jax
import jax.numpy as jnp
from jax import lax
from jax.sharding import PartitionSpec as P

CAP = 4


def from_behind(value, axis, by):
    devices = lax.axis_size(axis)
    pairs = [(i, i + by) for i in range(devices) if 0 <= i + by < devices]
    return lax.ppermute(value, axis, pairs)


def project(weight, row_data):
    return lax.dot_general(
        weight, row_data, (((1,), (1,)), ((), ())), preferred_element_type=jnp.float32
    )


def contract_units(columns, weight):
    return lax.dot_general(
        columns, weight, (((0,), (0,)), ((), ())), preferred_element_type=jnp.float32
    )


def on_device(saved_inputs, expert_ids, gate_weights, out_grad, gate_w, up_w, down_w):
    sections = lax.axis_size("section")
    section_index = lax.axis_index("section")
    slot_total = lax.axis_size("ep") * CAP
    model_width = saved_inputs.shape[2]
    unit_rows = gate_w.shape[1]
    tokens = saved_inputs[0]
    routes = expert_ids[0]
    is_live = routes == 0
    live_count = jnp.sum(is_live.astype(jnp.int32), axis=1)
    pair_weight = jnp.sum(jnp.where(is_live, gate_weights[0], 0.0), axis=1)
    slot_index = jnp.cumsum(live_count) - live_count
    target = jnp.where(live_count == 1, slot_index, CAP)
    safe_slot = jnp.minimum(target, CAP - 1)
    selector = (target[None, :] == jnp.arange(CAP, dtype=jnp.int32)[:, None]).astype(jnp.bfloat16)
    w_gate = gate_w[0]
    w_up = up_w[0]
    w_down = down_w[0]

    def pack_rows(row_data):
        return jnp.dot(selector, row_data, preferred_element_type=jnp.float32).astype(jnp.bfloat16)

    x_rows = lax.all_gather(pack_rows(tokens), "ep", axis=0, tiled=True)
    gate_pre = project(w_gate, x_rows)
    up_pre = project(w_up, x_rows)
    sigmoid_gate = jax.nn.sigmoid(gate_pre)
    activated = gate_pre * sigmoid_gate
    hidden = (activated * up_pre).astype(jnp.bfloat16)

    def grads_of(y_rows):
        grad_hidden = project(w_down, y_rows)
        d_up = (grad_hidden * activated).astype(jnp.bfloat16)
        d_gate = (
            grad_hidden * up_pre * sigmoid_gate * (1.0 + gate_pre * (1.0 - sigmoid_gate))
        ).astype(jnp.bfloat16)
        return (d_gate, d_up)

    def no_grads(y_rows):
        return (
            jnp.zeros((unit_rows, slot_total), jnp.bfloat16),
            jnp.zeros((unit_rows, slot_total), jnp.bfloat16),
        )

    def weight_grads(d_gate, d_up, y_rows):
        return (
            jnp.dot(d_gate, x_rows, preferred_element_type=jnp.float32).astype(jnp.bfloat16),
            jnp.dot(d_up, x_rows, preferred_element_type=jnp.float32).astype(jnp.bfloat16),
            jnp.dot(hidden, y_rows, preferred_element_type=jnp.float32).astype(jnp.bfloat16),
        )

    stored = (
        jnp.zeros((unit_rows, model_width), jnp.bfloat16),
        jnp.zeros((unit_rows, model_width), jnp.bfloat16),
        jnp.zeros((unit_rows, model_width), jnp.bfloat16),
    )
    current = lax.all_gather(out_grad, "section", axis=1, tiled=True)
    result = jnp.zeros_like(current)
    for step_index in range(sections):
        active = section_index == sections - 1 - step_index
        scaled = (pair_weight[:, None] * current.astype(jnp.float32)).astype(jnp.bfloat16)
        y_rows = lax.all_gather(pack_rows(scaled), "ep", axis=0, tiled=True)
        d_gate, d_up = lax.cond(active, grads_of, no_grads, y_rows)

        def compute(start_row):
            return contract_units(d_gate, w_gate) + contract_units(d_up, w_up)

        def skipped(start_row):
            return jnp.zeros((lax.axis_size("ep") * CAP, model_width), jnp.float32)

        back_rows = lax.psum_scatter(
            lax.cond(active, compute, skipped, jnp.int32(0)), "ep", scatter_dimension=0, tiled=True
        )
        back_tokens = jnp.where(live_count[:, None] == 1, back_rows[safe_slot], 0.0)
        input_grad = (current.astype(jnp.float32) + back_tokens).astype(jnp.bfloat16)
        result = jnp.where(active, input_grad, result)
        stored = lax.cond(
            active, lambda kept: weight_grads(d_gate, d_up, y_rows), lambda kept: kept, stored
        )
        if step_index + 1 < sections:
            current = from_behind(result, "section", -1)
    return (result[None], stored[0][None], stored[1][None], stored[2][None])


def solution(mesh):
    placed = (
        P("section", "ep", None),
        P("section", "ep", None),
        P("section", "ep", None),
        P("ep", "section"),
        P("section", "ep", None),
        P("section", "ep", None),
        P("section", "ep", None),
    )
    return jax.shard_map(
        on_device,
        mesh=mesh,
        in_specs=placed,
        out_specs=(
            P("section", "ep", None),
            P("section", "ep", None),
            P("section", "ep", None),
            P("section", "ep", None),
        ),
        check_vma=False,
    )
```

profile of v0, /device:TPU:0, one launch (start us, length us, event | category | flops | bytes accessed | tf_op | source)
XLA Modules:
  0.0 278.1 jit_solution(5775934028725770359)
XLA Ops:
  7.2 0.0 copy-start
  7.2 0.0 all-gather.7.cloned.1.call-start
  7.2 0.8 convert_reduce_fusion
  8.0 0.1 copy.17
  8.2 0.2 reduce-window.4
  8.3 0.1 fusion.30
  8.5 2.1 fusion.4
  10.6 0.0 all-gather.7.cloned.1.call-update
  10.6 0.0 all-gather.5.cloned.1.call-start
  10.6 0.7 select_reduce_fusion
  11.3 2.2 fusion.3
  13.5 0.0 all-gather.5.cloned.1.call-update
  13.6 0.0 all-reduce.3.cloned.1.call-start
  13.6 54.2 %all-gather.7.cloned.1.call-done = bf16[32,4,4096]{2,1,0:T(4,128)(2,1)} async-done(((bf16[1,4,4096]{2,1,0:T(4,128)(2,1)}), bf16[32,4,4096]{2,1,0:T(4,128)(2,1)}) %all-gather.7.cloned.1.call-update) | async-done | bytes 1048592 | tf_op jit(solution)/shard_map/all_gather | solution.py:49
  67.8 1.3 reshape.70
  69.1 2.1 fusion.19
  71.3 0.0 copy-done
  71.3 0.6 fusion.22
  71.9 51.9 %all-gather.5.cloned.1.call-done = bf16[32,4,4096]{2,1,0:T(4,128)(2,1)} async-done(((bf16[1,4,4096]{2,1,0:T(4,128)(2,1)}), bf16[32,4,4096]{2,1,0:T(4,128)(2,1)}) %all-gather.5.cloned.1.call-update) | async-done | bytes 1048592 | tf_op jit(solution)/shard_map/all_gather | solution.py:87
  123.8 2.1 reshape.68
  126.0 2.5 multiply_convert_fusion.1
  128.4 0.0 copy-start.2
  128.4 0.5 fusion.7
  128.9 1.0 copy-done.2
  129.9 1.8 convolution_add_fusion
  131.7 0.0 all-reduce.3.cloned.1.call-update
  131.8 1.9 fusion
  133.6 0.0 copy-start.1
  133.6 1.9 fusion.1
  135.5 0.0 copy-done.1
  135.5 1.9 fusion.2
  137.4 128.1 %all-reduce.3.cloned.1.call-done = f32[128,4096]{1,0:T(8,128)} async-done(((f32[128,4096]{1,0:T(8,128)}), f32[128,4096]{1,0:T(8,128)}) %all-reduce.3.cloned.1.call-update) | async-done | bytes 2097168
  265.4 0.9 constant_dynamic-slice_fusion
  266.3 0.0 copy-start.3
  266.4 2.4 gather_fusion
  268.7 0.0 copy-done.3
  268.7 2.9 %fusion.25 = bf16[1,128,4096]{2,1,0:T(8,128)(2,1)} fusion(f32[128,4096]{1,0:T(8,128)} %gather_fusion, bf16[128,4096]{1,0:T(8,128)(2,1)S(1)} %copy-done.3, pred[128]{0:T(512)(128)(4,1)S(1)} %broadcast_compare_fusion.1), kind=kLoop, calls=%fused_computation.28 | loop fusion | flops 2097152 | bytes 4194432 | tf_op jit(solution)/shard_map/broadcast_in_dim | solution.py:107
  (3 shorter events, 0.0 us)
Async XLA Ops:
  7.2 64.1 %copy-start = (bf16[1,224,4096]{2,1,0:T(8,128)(2,1)S(1)}, bf16[1,224,4096]{2,1,0:T(8,128)(2,1)}, u32[]{:S(2)}) copy-start(bf16[1,224,4096]{2,1,0:T(8,128)(2,1)} %param.11) | copy-start | bytes 5505028
  7.2 60.6 %all-gather.7.cloned.1.call-start = ((), (), s32[]{:S(2)}) async-start(), calls=%async_computation.1 | async-start | bytes 1081344 | tf_op jit(solution)/shard_map/all_gather | solution.py:49
  10.6 113.2 %all-gather.5.cloned.1.call-start = ((), (), s32[]{:S(2)}) async-start(), calls=%async_computation | async-start | bytes 1081344 | tf_op jit(solution)/shard_map/all_gather | solution.py:87
  13.6 251.9 %all-reduce.3.cloned.1.call-start = ((), (), s32[]{:S(2)}) async-start(), calls=%async_computation.2 | async-start | bytes 4194304
  128.4 1.5 copy-start.2
  133.6 1.9 copy-start.1
  266.3 2.4 copy-start.3
Sparse Core Ops, SparseCore 0:
  11.4 56.3 all-gather.6
  71.2 52.5 all-gather.4
  131.8 133.5 all-reduce.2
where the time goes:
time: 279 us; the launch traced here: 278 us
  waiting for transfers between devices  234 us (84%)
  matrix products  17.4 us (6%)
  between operations  13.8 us (5%)
  local copies, waits for them, and re-layouts  7.89 us (3%)
  other arithmetic  4.72 us (2%)
    unnamed x4, waiting for transfers between devices  128 us
    all_gather x1, waiting for transfers between devices, on_device(): x_rows = lax.all_gather(pack_rows(tokens), 'ep', axis=0, tiled=True)  54.2 us
    all_gather x1, waiting for transfers between devices, on_device(): y_rows = lax.all_gather(pack_rows(scaled), 'ep', axis=0, tiled=True)  51.9 us
  transfers between devices with their start and end apart: 3, of which 3 were waited for; matrix products, arithmetic and copies ran while one was open for 5% of the time, Pallas kernels for 0%

commit v1 on v0

v1 whole, which is shorter than its diff:
```python
import functools

import jax
import jax.numpy as jnp
from jax import lax
from jax.experimental import pallas as pl
from jax.experimental.pallas import tpu as pltpu
from jax.sharding import PartitionSpec as P

CAP = 4
PAIR = 2 * CAP
CHUNKS = 2
MESH = pl.DeviceIdType.MESH
F32 = jnp.float32
BF16 = jnp.bfloat16


def from_behind(value, axis, by):
    devices = lax.axis_size(axis)
    pairs = [(i, i + by) for i in range(devices) if 0 <= i + by < devices]
    return lax.ppermute(value, axis, pairs)


def exchange_kernel(
    depth, routes_ref, share_ref, tokens_hbm, current_hbm, wg_hbm, wu_hbm, wd_hbm,
    back_ref, select_ref, dg_ref, du_ref, hidden_ref, x_hbm, y_hbm,
    tok, wg, wu, wd, packed, pair_in, zbuf, full, pre,
    psend, prem, pown, qsend, qrecv, hsend, hrecv, total, zsend, zrecv, back,
    load_sem, pair_send, pair_recv, z_send, z_recv, p_send, p_recv, q_send, q_recv, d_send, d_recv,
    out_sem, rd_send, rd_recv, rq_send, rq_recv, rp_send, rp_recv, rz_send, rz_recv, rb_send, rb_recv,
):
    me = lax.axis_index("ep")
    c = me % 2
    a = (me // 2) % 2
    b = (me // 4) % 2
    z = me // 8
    own = b * 2 + a
    flip_a = 1 - 2 * a
    flip_b = 2 - 4 * b
    step_p = (1 - c) * flip_a + c * flip_b
    step_q = c * flip_a + (1 - c) * flip_b
    near_p, near_q, near_pq = own + step_p, own + step_q, own + step_p + step_q
    mate = me + 1 - 2 * c
    dev_p, dev_q = me + 2 * step_p, me + 2 * step_q
    other = 1 - c

    def dev_z(d):
        return (z + d) % depth * 8 + me % 8

    half = full.shape[-1]
    rows = full.shape[-2]
    chunk = half // CHUNKS

    def remote(src, dst, send_sem, recv_sem, device):
        return pltpu.make_async_remote_copy(
            src_ref=src, dst_ref=dst, send_sem=send_sem, recv_sem=recv_sem,
            device_id={"ep": device}, device_id_type=MESH,
        )

    loads = [
        pltpu.make_async_copy(src, dst, load_sem.at[i])
        for i, (src, dst) in enumerate(
            [(tokens_hbm, tok.at[0]), (current_hbm, tok.at[1]), (wg_hbm, wg), (wu_hbm, wu), (wd_hbm, wd)]
        )
    ]
    for load in loads:
        load.start()

    barrier = pltpu.get_barrier_semaphore()
    peers = [mate, dev_p, dev_q] + [dev_z(d) for d in range(1, depth)]
    for peer in peers:
        pl.semaphore_signal(barrier, inc=1, device_id={"ep": peer}, device_id_type=MESH)

    live = (routes_ref[0:1, :] == 0) | (routes_ref[1:2, :] == 0)
    weight = jnp.where(routes_ref[0:1, :] == 0, share_ref[0:1, :], 0.0) + jnp.where(
        routes_ref[1:2, :] == 0, share_ref[1:2, :], 0.0
    )
    count = live.shape[1]
    live_f = live.astype(F32)
    before = (
        lax.broadcasted_iota(jnp.int32, (count, count), 0) < lax.broadcasted_iota(jnp.int32, (count, count), 1)
    ).astype(F32)
    slot = jnp.dot(
        jnp.broadcast_to(live_f, (PAIR, count)).astype(BF16), before.astype(BF16), preferred_element_type=F32
    )
    place = lax.broadcasted_iota(jnp.int32, (PAIR, count), 0) - c * CAP
    chosen = (
        (slot == place.astype(F32)) & (place >= 0) & (place < CAP) & (jnp.broadcast_to(live_f, (PAIR, count)) > 0.5)
    )
    select = chosen.astype(F32)
    select_ref[...] = select
    slot_weight = jnp.sum(select * weight, axis=1, keepdims=True)
    selector = select.astype(BF16)

    pl.semaphore_wait(barrier, len(peers))

    pair_copies = []
    for m in range(2):
        loads[m].wait()
        for h in range(2):
            picked = jnp.dot(selector, tok[m, :, h * half : (h + 1) * half], preferred_element_type=F32)
            if m == 1:
                picked = picked * slot_weight
            packed[m, h] = picked.astype(BF16)
        copy = remote(packed.at[m, other], pair_in.at[m], pair_send.at[m], pair_recv.at[m], mate)
        copy.start()
        pair_copies.append(copy)

    sent = list(pair_copies)
    z_copies = [[], []]
    for m in range(2):
        pair_copies[m].wait_recv()
        zbuf[m, z] = (packed[m, c].astype(F32) + pair_in[m].astype(F32)).astype(BF16)
        for d in range(1, depth):
            copy = remote(zbuf.at[m, z], zbuf.at[m, z], z_send.at[m, d], z_recv.at[m, d], dev_z(d))
            copy.start()
            z_copies[m].append(copy)
            sent.append(copy)

    p_copies, q_copies, d_copies = [None, None], [[], []], [[], []]

    def group(m, g):
        return full.at[m, c, g]

    def to_mate(m, i, g):
        copy = remote(group(m, g), group(m, g), d_send.at[m, i], d_recv.at[m, i], mate)
        copy.start()
        d_copies[m].append(copy)
        sent.append(copy)

    def to_q(m, i, g):
        copy = remote(group(m, g), group(m, g), q_send.at[m, i], q_recv.at[m, i], dev_q)
        copy.start()
        q_copies[m].append(copy)
        sent.append(copy)

    for m in range(2):
        for copy in z_copies[m]:
            copy.wait_recv()
        full[m, c, own] = jnp.concatenate([zbuf[m, i].astype(F32) for i in range(depth)], axis=0).astype(BF16)
        p_copies[m] = remote(group(m, own), group(m, own), p_send.at[m], p_recv.at[m], dev_p)
        p_copies[m].start()
        sent.append(p_copies[m])
        to_q(m, 0, own)
        to_mate(m, 0, own)
    for m in range(2):
        p_copies[m].wait_recv()
        to_q(m, 1, near_p)
        to_mate(m, 1, near_p)

    def finish(m):
        q_copies[m][0].wait_recv()
        to_mate(m, 2, near_q)
        q_copies[m][1].wait_recv()
        to_mate(m, 3, near_pq)

    def arrive(m):
        for copy in d_copies[m]:
            copy.wait_recv()

    tile = 512
    tiles = half // tile

    def project(weights, m):
        def body(t, value):
            for h in range(2):
                start = pl.multiple_of(t * tile, tile)
                data = full[m, h, :, :, pl.ds(start, tile)].reshape(4 * rows, tile)
                value = value + lax.dot_general(
                    weights[:, pl.ds(pl.multiple_of(h * half + t * tile, tile), tile)], data,
                    (((1,), (1,)), ((), ())), preferred_element_type=F32,
                )
            return value

        return lax.fori_loop(0, tiles, body, jnp.zeros((weights.shape[0], 4 * rows), F32))

    finish(0)
    arrive(0)
    loads[2].wait()
    pre[0] = project(wg, 0)
    finish(1)
    loads[3].wait()
    pre[1] = project(wu, 0)
    loads[4].wait()
    arrive(1)
    outs = [
        pltpu.make_async_copy(full.at[0], x_hbm, out_sem.at[0]),
        pltpu.make_async_copy(full.at[1], y_hbm, out_sem.at[1]),
    ]
    for out in outs:
        out.start()
    grad_hidden = project(wd, 1)
    gate_pre, up_pre = pre[0], pre[1]
    sig = jax.nn.sigmoid(gate_pre)
    act = gate_pre * sig
    hidden_ref[...] = (act * up_pre).astype(BF16)
    du_ref[...] = (grad_hidden * act).astype(BF16)
    dg_ref[...] = (grad_hidden * up_pre * sig * (1.0 + gate_pre * (1.0 - sig))).astype(BF16)

    wide = min(512, chunk)

    def contract(h, k, store):
        def body(t, carry):
            inner = pl.multiple_of(t * wide, wide)
            start = pl.multiple_of(h * half + k * chunk + t * wide, wide)
            dims = (((0,), (0,)), ((), ()))
            part = lax.dot_general(dg_ref[...], wg[:, pl.ds(start, wide)], dims, preferred_element_type=F32)
            part += lax.dot_general(du_ref[...], wu[:, pl.ds(start, wide)], dims, preferred_element_type=F32)
            store(pl.ds(inner, wide), part.reshape(4, rows, wide))
            return carry

        lax.fori_loop(0, chunk // wide, body, 0)

    rd, rq, rp, rz, rb = [], [], [], [], []
    for k in range(CHUNKS):
        def store_send(cols, part, k=k):
            psend[k, :, :, cols] = part.astype(BF16)

        contract(other, k, store_send)
        copy = remote(psend.at[k], prem.at[k], rd_send.at[k], rd_recv.at[k], mate)
        copy.start()
        rd.append(copy)
    for k in range(CHUNKS):
        def store_own(cols, part, k=k):
            pown[k, :, :, cols] = part

        contract(c, k, store_own)
    for k in range(CHUNKS):
        rd[k].wait_recv()
        pair = []
        for i, g in enumerate((near_pq, near_q)):
            qsend[k, i] = (pown[k, g] + prem[k, g].astype(F32)).astype(BF16)
            copy = remote(qsend.at[k, i], qrecv.at[k, i], rq_send.at[k, i], rq_recv.at[k, i], dev_q)
            copy.start()
            pair.append(copy)
        rq.append(pair)
    for k in range(CHUNKS):
        rq[k][0].wait_recv()
        hsend[k] = (pown[k, near_p] + prem[k, near_p].astype(F32) + qrecv[k, 0].astype(F32)).astype(BF16)
        copy = remote(hsend.at[k], hrecv.at[k], rp_send.at[k], rp_recv.at[k], dev_p)
        copy.start()
        rp.append(copy)
    for k in range(CHUNKS):
        rq[k][1].wait_recv()
        mine = pown[k, own] + prem[k, own].astype(F32) + qrecv[k, 1].astype(F32)
        rp[k].wait_recv()
        total[k] = (mine + hrecv[k].astype(F32)).reshape(depth, PAIR, chunk)
        some = []
        for d in range(1, depth):
            zsend[k, d] = total[k, (z + d) % depth].astype(BF16)
            copy = remote(zsend.at[k, d], zrecv.at[k, d], rz_send.at[k, d], rz_recv.at[k, d], dev_z(d))
            copy.start()
            some.append(copy)
        rz.append(some)
    for k in range(CHUNKS):
        value = total[k, z]
        for d in range(1, depth):
            rz[k][d - 1].wait_recv()
            value = value + zrecv[k, d].astype(F32)
        back[c, k] = value
        copy = remote(back.at[c, k], back.at[c, k], rb_send.at[k], rb_recv.at[k], mate)
        copy.start()
        rb.append(copy)
    for k in range(CHUNKS):
        rb[k].wait_recv()
    back_ref[...] = back[...]
    for copy in sent + rd + rp + rb + sum(rq, []) + sum(rz, []):
        copy.wait_send()
    for out in outs:
        out.wait()


def exchange(routes, shares, tokens, current, w_gate, w_up, w_down, devices):
    depth = devices // 8
    count, width = tokens.shape
    units = w_gate.shape[0]
    half = width // 2
    chunk = half // CHUNKS
    rows = depth * PAIR
    slots = devices * CAP
    dma = pltpu.SemaphoreType.DMA
    vmem = pl.BlockSpec(memory_space=pltpu.VMEM)
    hbm = pl.BlockSpec(memory_space=pl.ANY)
    return pl.pallas_call(
        functools.partial(exchange_kernel, depth),
        out_shape=(
            jax.ShapeDtypeStruct((2, CHUNKS, PAIR, chunk), F32),
            jax.ShapeDtypeStruct((PAIR, count), F32),
            jax.ShapeDtypeStruct((units, slots), BF16),
            jax.ShapeDtypeStruct((units, slots), BF16),
            jax.ShapeDtypeStruct((units, slots), BF16),
            jax.ShapeDtypeStruct((2, 4, rows, half), BF16),
            jax.ShapeDtypeStruct((2, 4, rows, half), BF16),
        ),
        in_specs=[vmem, vmem] + [hbm] * 5,
        out_specs=(vmem,) * 5 + (hbm,) * 2,
        scratch_shapes=[
            pltpu.VMEM((2, count, width), BF16),
            pltpu.VMEM((units, width), BF16),
            pltpu.VMEM((units, width), BF16),
            pltpu.VMEM((units, width), BF16),
            pltpu.VMEM((2, 2, PAIR, half), BF16),
            pltpu.VMEM((2, PAIR, half), BF16),
            pltpu.VMEM((2, depth, PAIR, half), BF16),
            pltpu.VMEM((2, 2, 4, rows, half), BF16),
            pltpu.VMEM((2, units, slots), F32),
            pltpu.VMEM((CHUNKS, 4, rows, chunk), BF16),
            pltpu.VMEM((CHUNKS, 4, rows, chunk), BF16),
            pltpu.VMEM((CHUNKS, 4, rows, chunk), F32),
            pltpu.VMEM((CHUNKS, 2, rows, chunk), BF16),
            pltpu.VMEM((CHUNKS, 2, rows, chunk), BF16),
            pltpu.VMEM((CHUNKS, rows, chunk), BF16),
            pltpu.VMEM((CHUNKS, rows, chunk), BF16),
            pltpu.VMEM((CHUNKS, depth, PAIR, chunk), F32),
            pltpu.VMEM((CHUNKS, depth, PAIR, chunk), BF16),
            pltpu.VMEM((CHUNKS, depth, PAIR, chunk), BF16),
            pltpu.VMEM((2, CHUNKS, PAIR, chunk), F32),
            dma((5,)), dma((2,)), dma((2,)), dma((2, depth)), dma((2, depth)), dma((2,)), dma((2,)),
            dma((2, 2)), dma((2, 2)), dma((2, 4)), dma((2, 4)), dma((2,)),
            dma((CHUNKS,)), dma((CHUNKS,)), dma((CHUNKS, 2)), dma((CHUNKS, 2)),
            dma((CHUNKS,)), dma((CHUNKS,)), dma((CHUNKS, depth)), dma((CHUNKS, depth)),
            dma((CHUNKS,)), dma((CHUNKS,)),
        ],
        compiler_params=pltpu.CompilerParams(
            collective_id=0, has_side_effects=True, vmem_limit_bytes=56 * 1024 * 1024
        ),
        name="exchange",
    )(routes, shares, tokens, current, w_gate, w_up, w_down)


def outputs_kernel(back_ref, select_ref, dg_ref, du_ref, hidden_ref, x_ref, y_ref, current_ref,
                   input_ref, gate_ref, up_ref, down_ref):
    slots = dg_ref.shape[1]
    x_rows = x_ref[0].reshape(slots, x_ref.shape[-1])
    y_rows = y_ref[0].reshape(slots, y_ref.shape[-1])
    gate_ref[...] = jnp.dot(dg_ref[...], x_rows, preferred_element_type=F32).astype(BF16)
    up_ref[...] = jnp.dot(du_ref[...], x_rows, preferred_element_type=F32).astype(BF16)
    down_ref[...] = jnp.dot(hidden_ref[...], y_rows, preferred_element_type=F32).astype(BF16)
    spread = lax.dot_general(
        select_ref[...], back_ref[0, 0], (((0,), (0,)), ((), ())),
        preferred_element_type=F32, precision=lax.Precision.HIGHEST,
    )
    input_ref[...] = (current_ref[...].astype(F32) + spread).astype(BF16)


def outputs(back, select, d_gate, d_up, hidden, x_rows, y_rows, current):
    count, width = current.shape
    units, slots = d_gate.shape
    half = width // 2
    tile = 512
    per_half = half // tile
    per_chunk = back.shape[-1] // tile
    whole = lambda t: (0, 0)
    columns = lambda t: (0, t)
    data = pl.BlockSpec((1,) + x_rows.shape[1:3] + (tile,), lambda t: (t // per_half, 0, 0, t % per_half))
    return pl.pallas_call(
        outputs_kernel,
        grid=(width // tile,),
        out_shape=(
            jax.ShapeDtypeStruct((count, width), BF16),
            jax.ShapeDtypeStruct((units, width), BF16),
            jax.ShapeDtypeStruct((units, width), BF16),
            jax.ShapeDtypeStruct((units, width), BF16),
        ),
        in_specs=[
            pl.BlockSpec(
                (1, 1, PAIR, tile),
                lambda t: (t // per_half, t % per_half // per_chunk, 0, t % per_chunk),
            ),
            pl.BlockSpec((PAIR, count), whole),
            pl.BlockSpec((units, slots), whole),
            pl.BlockSpec((units, slots), whole),
            pl.BlockSpec((units, slots), whole),
            data,
            data,
            pl.BlockSpec((count, tile), columns),
        ],
        out_specs=(
            pl.BlockSpec((count, tile), columns),
            pl.BlockSpec((units, tile), columns),
            pl.BlockSpec((units, tile), columns),
            pl.BlockSpec((units, tile), columns),
        ),
        name="outputs",
    )(back, select, d_gate, d_up, hidden, x_rows, y_rows, current)


def on_device(saved_inputs, expert_ids, gate_weights, out_grad, gate_w, up_w, down_w):
    sections = lax.axis_size("section")
    section_index = lax.axis_index("section")
    devices = lax.axis_size("ep")
    routes = expert_ids[0].T
    shares = gate_weights[0].T
    current = out_grad if sections == 1 else lax.all_gather(out_grad, "section", axis=1, tiled=True)
    kept = None
    for step_index in range(sections):
        active = section_index == sections - 1 - step_index
        parts = exchange(routes, shares, saved_inputs[0], current, gate_w[0], up_w[0], down_w[0], devices)
        made = outputs(*parts, current)
        kept = made if kept is None else tuple(jnp.where(active, new, old) for new, old in zip(made, kept))
        if step_index + 1 < sections:
            current = from_behind(made[0], "section", -1)
    return tuple(value[None] for value in kept)


def solution(mesh):
    placed = (
        P("section", "ep", None),
        P("section", "ep", None),
        P("section", "ep", None),
        P("ep", "section"),
        P("section", "ep", None),
        P("section", "ep", None),
        P("section", "ep", None),
    )
    return jax.shard_map(
        on_device,
        mesh=mesh,
        in_specs=placed,
        out_specs=(
            P("section", "ep", None),
            P("section", "ep", None),
            P("section", "ep", None),
            P("section", "ep", None),
        ),
        check_vma=False,
    )
```

time: 279 us -> 51.1 us (0.18)
  waiting for transfers between devices: 234 us -> 0 us
  Pallas kernels: 0 us -> 50.2 us
  matrix products: 17.4 us -> 0 us
  between operations: 13.8 us -> 0.64 us
  local copies, waits for them, and re-layouts: 7.89 us -> 0 us
  other arithmetic: 4.72 us -> 0 us
    unnamed x4 -> x0, waiting for transfers between devices: 128 us -> none
    all_gather x2 -> x0, waiting for transfers between devices: 106 us -> none  [the longest x1 54.2 us: on_device(): x_rows = lax.all_gather(pack_rows(tokens), 'ep', axis=0, tiled=True)]
    pallas_call x0 -> x2, Pallas kernels: none -> 50.2 us  [the longest x1 42.2 us: exchange(): pl.pallas_call(functools.partial(exchange_kernel, depth), out_shape=(jax....]
    dot_general x10 -> x0, matrix products: 17.4 us -> none  [the longest x3 5.23 us: project(): lax.dot_general(weight, row_data, (((1,), (1,)), ((), ())), preferred_ele...]
    unnamed x11 -> x0, local copies, waits for them, and re-layouts: 5.41 us -> none
    broadcast_in_dim x1 -> x0, other arithmetic: 2.89 us -> none  [on_device(): return (result[None], stored[0][None], stored[1][None], stored[2][None])]
  transfers between devices with their start and end apart: 3 -> 0, of which waited for: 3 -> 0; matrix products, arithmetic and copies ran while one was open for 5% -> 0% of each run, Pallas kernels for 0% -> 0%
where the time goes in v1:
time: 51.1 us; the launch traced here: 50.9 us
  Pallas kernels  50.2 us (98%)
  between operations  0.64 us (1%)
    pallas_call x1, Pallas kernels, exchange(): pl.pallas_call(functools.partial(exchange_kernel, depth), out_shape=(jax....  42.2 us
    pallas_call x1, Pallas kernels, outputs(): pl.pallas_call(outputs_kernel, grid=(width // tile,), out_shape=(jax.Shap...  7.99 us

profile of v1, /device:TPU:0, one launch (start us, length us, event | category | flops | bytes accessed | tf_op | source)
XLA Modules:
  0.0 50.9 jit_solution(4468143246668235917)
XLA Ops:
  0.6 42.2 %exchange.1 = (f32[2,2,8,1024]{3,2,1,0:T(8,128)}, f32[8,128]{1,0:T(8,128)}, bf16[224,128]{1,0:T(8,128)(2,1)}, bf16[224,128]{1,0:T(8,128)(2,1)}, bf16[224,128]{1,...) custom-call(s32[2,128]{1,0:T(2,128)} %bitcast.18, f32[2,128]{1,0:T(2,128)} %bitcast.19, ...), custom_call_target="tpu_custom_call" | custom-call | tf_op jit(solution)/shard_map/exchange/pallas_call | solution.py:284
  42.9 8.0 %outputs.1 = (bf16[128,4096]{1,0:T(8,128)(2,1)}, bf16[224,4096]{1,0:T(8,128)(2,1)}, bf16[224,4096]{1,0:T(8,128)(2,1)}, bf16[224,4096]{1,0:T(8,128)(2,1)}) custom-call(f32[2,2,8,1024]{3,2,1,0:T(8,128)} %get-tuple-element.15.back_ref, f32[8,128]{1,0:T(8,128)} %get-tuple-element.16.select_ref, bf16[224,128]{1,0:T(8,128)(2,1)} %get-tuple-element.17.dg_ref, ...), custom_call_target="tpu_custom_call" | custom-call | tf_op jit(solution)/shard_map/outputs/pallas_call | solution.py:356

commit v2 on v1

v2 whole, which is shorter than its diff:
```python
import functools

import jax
import jax.numpy as jnp
from jax import lax
from jax.experimental import pallas as pl
from jax.experimental.pallas import tpu as pltpu
from jax.sharding import PartitionSpec as P

CAP = 4
CHUNKS = 2
MESH = pl.DeviceIdType.MESH
F32 = jnp.float32
BF16 = jnp.bfloat16


def from_behind(value, axis, by):
    devices = lax.axis_size(axis)
    pairs = [(i, i + by) for i in range(devices) if 0 <= i + by < devices]
    return lax.ppermute(value, axis, pairs)


def exchange_kernel(
    depth, routes_hbm, share_hbm, tokens_hbm, current_hbm, wg_hbm, wu_hbm, wd_hbm,
    back_ref, select_ref, gate_ref, up_ref, down_ref,
    routes_ref, share_ref, dg_ref, du_ref, hidden_ref, tok, wg, wu, wd, packed, zbuf, full, pre,
    psend, prem, pown, qsend, qrecv, hsend, hrecv, total, zsend, zrecv,
    load_sem, z_send, z_recv, p_send, p_recv, q_send, q_recv, d_send, d_recv,
    rd_send, rd_recv, rq_send, rq_recv, rp_send, rp_recv, rz_send, rz_recv,
):
    me = lax.axis_index("ep")
    c = me % 2
    a = (me // 2) % 2
    b = (me // 4) % 2
    z = me // 8
    own = b * 2 + a
    flip_a = 1 - 2 * a
    flip_b = 2 - 4 * b
    step_p = (1 - c) * flip_a + c * flip_b
    step_q = c * flip_a + (1 - c) * flip_b
    near_p, near_q, near_pq = own + step_p, own + step_q, own + step_p + step_q
    mate = me + 1 - 2 * c
    dev_p, dev_q = me + 2 * step_p, me + 2 * step_q
    other = 1 - c

    def dev_z(d, core):
        return (z + d) % depth * 8 + own * 2 + core

    half = full.shape[-1]
    rows = full.shape[-2]
    chunk = half // CHUNKS

    def remote(src, dst, send_sem, recv_sem, device):
        return pltpu.make_async_remote_copy(
            src_ref=src, dst_ref=dst, send_sem=send_sem, recv_sem=recv_sem,
            device_id={"ep": device}, device_id_type=MESH,
        )

    loads = [
        pltpu.make_async_copy(src, dst, load_sem.at[i])
        for i, (src, dst) in enumerate(
            [
                (tokens_hbm, tok.at[0]), (current_hbm, tok.at[1]), (wg_hbm, wg), (wu_hbm, wu), (wd_hbm, wd),
                (routes_hbm, routes_ref), (share_hbm, share_ref),
            ]
        )
    ]
    for load in loads[5:] + loads[:5]:
        load.start()

    barrier = pltpu.get_barrier_semaphore()
    peers = [mate, dev_p, dev_q] + [dev_z(d, h) for d in range(1, depth) for h in range(2)]
    for peer in peers:
        pl.semaphore_signal(barrier, inc=1, device_id={"ep": peer}, device_id_type=MESH)

    loads[5].wait()
    loads[6].wait()
    live = (routes_ref[0:1, :] == 0) | (routes_ref[1:2, :] == 0)
    weight = jnp.where(routes_ref[0:1, :] == 0, share_ref[0:1, :], 0.0) + jnp.where(
        routes_ref[1:2, :] == 0, share_ref[1:2, :], 0.0
    )
    count = live.shape[1]
    live_f = live.astype(F32)
    before = (
        lax.broadcasted_iota(jnp.int32, (count, count), 0) < lax.broadcasted_iota(jnp.int32, (count, count), 1)
    ).astype(F32)
    slot = jnp.dot(
        jnp.broadcast_to(live_f, (CAP, count)).astype(BF16), before.astype(BF16), preferred_element_type=F32
    )
    place = lax.broadcasted_iota(jnp.int32, (CAP, count), 0)
    chosen = (
        (slot == place.astype(F32)) & (jnp.broadcast_to(live_f, (CAP, count)) > 0.5)
    )
    select = chosen.astype(F32)
    select_ref[...] = select
    slot_weight = jnp.sum(select * weight, axis=1, keepdims=True)
    selector = select.astype(BF16)

    pl.semaphore_wait(barrier, len(peers))

    sent = []
    z_copies = [[], []]
    for m in range(2):
        loads[m].wait()
        for h in range(2):
            picked = jnp.dot(selector, tok[m, :, h * half : (h + 1) * half], preferred_element_type=F32)
            if m == 1:
                picked = picked * slot_weight
            packed[m, h] = picked.astype(BF16)
        for d in range(1, depth):
            for h in range(2):
                z_copies[m].append(
                    remote(packed.at[m, h], zbuf.at[m, z, c], z_send.at[m, d, h], z_recv.at[m, d, c], dev_z(d, h))
                )
        z_copies[m].append(
            remote(packed.at[m, other], zbuf.at[m, z, c], z_send.at[m, 0, 0], z_recv.at[m, 0, 0], mate)
        )
        for copy in z_copies[m]:
            copy.start()
        sent += z_copies[m]
        zbuf[m, z, c] = packed[m, c]

    def from_z(m):
        for d in range(1, depth):
            for h in range(2):
                remote(packed.at[m, h], zbuf.at[m, z, c], z_send.at[m, d, h], z_recv.at[m, d, h], mate).wait_recv()
        z_copies[m][-1].wait_recv()

    p_copies, q_copies, d_copies = [None, None], [[], []], [[], []]

    def group(m, g):
        return full.at[m, c, g]

    def to_mate(m, i, g):
        copy = remote(group(m, g), group(m, g), d_send.at[m, i], d_recv.at[m, i], mate)
        copy.start()
        d_copies[m].append(copy)
        sent.append(copy)

    def to_q(m, i, g):
        copy = remote(group(m, g), group(m, g), q_send.at[m, i], q_recv.at[m, i], dev_q)
        copy.start()
        q_copies[m].append(copy)
        sent.append(copy)

    for m in range(2):
        from_z(m)
        full[m, c, own] = jnp.concatenate(
            [zbuf[m, i, h].astype(F32) for i in range(depth) for h in range(2)], axis=0
        ).astype(BF16)
        p_copies[m] = remote(group(m, own), group(m, own), p_send.at[m], p_recv.at[m], dev_p)
        p_copies[m].start()
        sent.append(p_copies[m])
        to_q(m, 0, own)
        to_mate(m, 0, own)
    for m in range(2):
        p_copies[m].wait_recv()
        to_q(m, 1, near_p)
        to_mate(m, 1, near_p)

    def finish(m):
        q_copies[m][0].wait_recv()
        to_mate(m, 2, near_q)
        q_copies[m][1].wait_recv()
        to_mate(m, 3, near_pq)

    def arrive(m):
        for copy in d_copies[m]:
            copy.wait_recv()

    tile = 512
    tiles = half // tile

    def project(weights, m, h, value):
        def body(t, value):
            start = pl.multiple_of(t * tile, tile)
            data = full[m, h, :, :, pl.ds(start, tile)].reshape(4 * rows, tile)
            return value + lax.dot_general(
                weights[:, pl.ds(pl.multiple_of(h * half + t * tile, tile), tile)], data,
                (((1,), (1,)), ((), ())), preferred_element_type=F32,
            )

        return lax.fori_loop(0, tiles, body, value)

    def weight_grad(out_ref, left_ref, m):
        left = left_ref[...]
        for h in range(2):
            def body(t, carry):
                data = full[m, h, :, :, pl.ds(pl.multiple_of(t * tile, tile), tile)].reshape(4 * rows, tile)
                cols = pl.ds(pl.multiple_of(h * half + t * tile, tile), tile)
                out_ref[:, cols] = jnp.dot(left, data, preferred_element_type=F32).astype(BF16)
                return carry

            lax.fori_loop(0, tiles, body, 0)

    zero = jnp.zeros((wg.shape[0], 4 * rows), F32)
    finish(0)
    loads[2].wait()
    pre[0] = project(wg, 0, c, zero)
    arrive(0)
    pre[0] = project(wg, 0, other, pre[0])
    loads[3].wait()
    pre[1] = project(wu, 0, c, zero)
    finish(1)
    loads[4].wait()
    pre[1] = project(wu, 0, other, pre[1])
    grad_hidden = project(wd, 1, c, zero)
    arrive(1)
    grad_hidden = project(wd, 1, other, grad_hidden)
    gate_pre, up_pre = pre[0], pre[1]
    sig = jax.nn.sigmoid(gate_pre)
    act = gate_pre * sig
    hidden_ref[...] = (act * up_pre).astype(BF16)
    du_ref[...] = (grad_hidden * act).astype(BF16)
    dg_ref[...] = (grad_hidden * up_pre * sig * (1.0 + gate_pre * (1.0 - sig))).astype(BF16)

    wide = min(512, chunk)

    def contract(h, k, store):
        def body(t, carry):
            inner = pl.multiple_of(t * wide, wide)
            start = pl.multiple_of(h * half + k * chunk + t * wide, wide)
            dims = (((0,), (0,)), ((), ()))
            part = lax.dot_general(dg_ref[...], wg[:, pl.ds(start, wide)], dims, preferred_element_type=F32)
            part += lax.dot_general(du_ref[...], wu[:, pl.ds(start, wide)], dims, preferred_element_type=F32)
            store(pl.ds(inner, wide), part.reshape(4, rows, wide))
            return carry

        lax.fori_loop(0, chunk // wide, body, 0)

    rd, rq, rp, rz = [], [], [], []
    for k in range(CHUNKS):
        def store_send(cols, part, k=k):
            psend[k, :, :, cols] = part.astype(BF16)

        contract(other, k, store_send)
        copy = remote(psend.at[k], prem.at[k], rd_send.at[k], rd_recv.at[k], mate)
        copy.start()
        rd.append(copy)
    for k in range(CHUNKS):
        def store_own(cols, part, k=k):
            pown[k, :, :, cols] = part

        contract(c, k, store_own)
    for k in range(CHUNKS):
        rd[k].wait_recv()
        pair = []
        for i, g in enumerate((near_pq, near_q)):
            qsend[k, i] = (pown[k, g] + prem[k, g].astype(F32)).astype(BF16)
            copy = remote(qsend.at[k, i], qrecv.at[k, i], rq_send.at[k, i], rq_recv.at[k, i], dev_q)
            copy.start()
            pair.append(copy)
        rq.append(pair)
    weight_grad(gate_ref, dg_ref, 0)
    for k in range(CHUNKS):
        rq[k][0].wait_recv()
        hsend[k] = (pown[k, near_p] + prem[k, near_p].astype(F32) + qrecv[k, 0].astype(F32)).astype(BF16)
        copy = remote(hsend.at[k], hrecv.at[k], rp_send.at[k], rp_recv.at[k], dev_p)
        copy.start()
        rp.append(copy)
    weight_grad(up_ref, du_ref, 0)
    for k in range(CHUNKS):
        rq[k][1].wait_recv()
        mine = pown[k, own] + prem[k, own].astype(F32) + qrecv[k, 1].astype(F32)
        rp[k].wait_recv()
        mine = mine + hrecv[k].astype(F32)
        for i in range(depth):
            for h in range(2):
                start = (2 * i + h) * CAP
                total[k, i, h] = mine[start : start + CAP]
        some = []
        for d in range(1, depth):
            for h in range(2):
                zsend[k, d, h] = total[k, (z + d) % depth, h].astype(BF16)
                some.append(
                    remote(zsend.at[k, d, h], zrecv.at[k, d, c], rz_send.at[k, d, h], rz_recv.at[k, d, c], dev_z(d, h))
                )
                some[-1].start()
        zsend[k, 0, 0] = total[k, z, other].astype(BF16)
        some.append(remote(zsend.at[k, 0, 0], zrecv.at[k, 0, c], rz_send.at[k, 0, 0], rz_recv.at[k, 0, 0], mate))
        some[-1].start()
        rz.append(some)
    weight_grad(down_ref, hidden_ref, 1)
    for k in range(CHUNKS):
        for d in range(1, depth):
            for h in range(2):
                remote(
                    zsend.at[k, d, h], zrecv.at[k, d, h], rz_send.at[k, d, h], rz_recv.at[k, d, h], mate
                ).wait_recv()
        rz[k][-1].wait_recv()
        back_ref[c, k] = total[k, z, c] + sum(zrecv[k, d, c].astype(F32) for d in range(1, depth))
        back_ref[other, k] = sum(zrecv[k, d, other].astype(F32) for d in range(depth))
    for copy in sent + rd + rp + sum(rq, []) + sum(rz, []):
        copy.wait_send()


def exchange(routes, shares, tokens, current, w_gate, w_up, w_down, devices):
    depth = devices // 8
    count, width = tokens.shape
    units = w_gate.shape[0]
    operands = (routes, shares, tokens, current, w_gate, w_up, w_down)
    half = width // 2
    chunk = half // CHUNKS
    rows = depth * 2 * CAP
    slots = devices * CAP
    dma = pltpu.SemaphoreType.DMA
    vmem = pl.BlockSpec(memory_space=pltpu.VMEM)
    hbm = pl.BlockSpec(memory_space=pltpu.HBM)
    return pl.pallas_call(
        functools.partial(exchange_kernel, depth),
        out_shape=(
            jax.ShapeDtypeStruct((2, CHUNKS, CAP, chunk), F32),
            jax.ShapeDtypeStruct((CAP, count), F32),
            jax.ShapeDtypeStruct((units, width), BF16),
            jax.ShapeDtypeStruct((units, width), BF16),
            jax.ShapeDtypeStruct((units, width), BF16),
        ),
        in_specs=[hbm] * 7,
        out_specs=(vmem,) * 5,
        scratch_shapes=[
            pltpu.VMEM(routes.shape, jnp.int32),
            pltpu.VMEM(shares.shape, F32),
            pltpu.VMEM((units, slots), BF16),
            pltpu.VMEM((units, slots), BF16),
            pltpu.VMEM((units, slots), BF16),
            pltpu.VMEM((2, count, width), BF16),
            pltpu.VMEM((units, width), BF16),
            pltpu.VMEM((units, width), BF16),
            pltpu.VMEM((units, width), BF16),
            pltpu.VMEM((2, 2, CAP, half), BF16),
            pltpu.VMEM((2, depth, 2, CAP, half), BF16),
            pltpu.VMEM((2, 2, 4, rows, half), BF16),
            pltpu.VMEM((2, units, slots), F32),
            pltpu.VMEM((CHUNKS, 4, rows, chunk), BF16),
            pltpu.VMEM((CHUNKS, 4, rows, chunk), BF16),
            pltpu.VMEM((CHUNKS, 4, rows, chunk), F32),
            pltpu.VMEM((CHUNKS, 2, rows, chunk), BF16),
            pltpu.VMEM((CHUNKS, 2, rows, chunk), BF16),
            pltpu.VMEM((CHUNKS, rows, chunk), BF16),
            pltpu.VMEM((CHUNKS, rows, chunk), BF16),
            pltpu.VMEM((CHUNKS, depth, 2, CAP, chunk), F32),
            pltpu.VMEM((CHUNKS, depth, 2, CAP, chunk), BF16),
            pltpu.VMEM((CHUNKS, depth, 2, CAP, chunk), BF16),
            dma((7,)), dma((2, depth, 2)), dma((2, depth, 2)), dma((2,)), dma((2,)),
            dma((2, 2)), dma((2, 2)), dma((2, 4)), dma((2, 4)),
            dma((CHUNKS,)), dma((CHUNKS,)), dma((CHUNKS, 2)), dma((CHUNKS, 2)),
            dma((CHUNKS,)), dma((CHUNKS,)), dma((CHUNKS, depth, 2)), dma((CHUNKS, depth, 2)),
        ],
        compiler_params=pltpu.CompilerParams(
            collective_id=0, has_side_effects=True, vmem_limit_bytes=28 * 1024 * 1024
        ),
        name="exchange",
    )(*[pltpu.with_memory_space_constraint(v, pltpu.HBM) for v in operands])


def outputs_kernel(back_ref, select_ref, gate_ref, up_ref, down_ref, current_hbm,
                   input_hbm, gate_hbm, up_hbm, down_hbm, held, made, load_sem, store_sem):
    parts = 2 * CHUNKS
    tile = held.shape[1] // parts
    loads, stores = [], []
    for i in range(parts):
        cols = pl.ds(i * tile, tile)
        loads.append(pltpu.make_async_copy(current_hbm.at[:, cols], held.at[:, cols], load_sem.at[i]))
        loads[-1].start()
    for i, (src, dst) in enumerate([(gate_ref, gate_hbm), (up_ref, up_hbm), (down_ref, down_hbm)]):
        stores.append(pltpu.make_async_copy(src, dst, store_sem.at[i]))
        stores[-1].start()
    for i in range(parts):
        cols = pl.ds(i * tile, tile)
        spread = lax.dot_general(
            select_ref[...], back_ref[i // CHUNKS, i % CHUNKS], (((0,), (0,)), ((), ())),
            preferred_element_type=F32, precision=lax.Precision.HIGHEST,
        )
        loads[i].wait()
        made[:, cols] = (held[:, cols].astype(F32) + spread).astype(BF16)
        stores.append(pltpu.make_async_copy(made.at[:, cols], input_hbm.at[:, cols], store_sem.at[3 + i]))
        stores[-1].start()
    for store in stores:
        store.wait()


def outputs(back, select, grad_gate, grad_up, grad_down, current):
    vmem = pl.BlockSpec(memory_space=pltpu.VMEM)
    hbm = pl.BlockSpec(memory_space=pltpu.HBM)
    shape = jax.ShapeDtypeStruct(grad_gate.shape, BF16)
    return pl.pallas_call(
        outputs_kernel,
        out_shape=(jax.ShapeDtypeStruct(current.shape, BF16), shape, shape, shape),
        in_specs=[vmem] * 5 + [hbm],
        out_specs=(hbm,) * 4,
        scratch_shapes=[
            pltpu.VMEM(current.shape, BF16),
            pltpu.VMEM(current.shape, BF16),
            pltpu.SemaphoreType.DMA((2 * CHUNKS,)),
            pltpu.SemaphoreType.DMA((3 + 2 * CHUNKS,)),
        ],
        compiler_params=pltpu.CompilerParams(vmem_limit_bytes=16 * 1024 * 1024),
        name="outputs",
    )(back, select, grad_gate, grad_up, grad_down, current)


def on_device(saved_inputs, expert_ids, gate_weights, out_grad, gate_w, up_w, down_w):
    sections = lax.axis_size("section")
    section_index = lax.axis_index("section")
    devices = lax.axis_size("ep")
    routes = expert_ids[0].T
    shares = gate_weights[0].T
    current = out_grad if sections == 1 else lax.all_gather(out_grad, "section", axis=1, tiled=True)
    kept = None
    for step_index in range(sections):
        active = section_index == sections - 1 - step_index
        parts = exchange(routes, shares, saved_inputs[0], current, gate_w[0], up_w[0], down_w[0], devices)
        made = outputs(*parts, current)
        kept = made if kept is None else tuple(jnp.where(active, new, old) for new, old in zip(made, kept))
        if step_index + 1 < sections:
            current = from_behind(made[0], "section", -1)
    return tuple(value[None] for value in kept)


def solution(mesh):
    placed = (
        P("section", "ep", None),
        P("section", "ep", None),
        P("section", "ep", None),
        P("ep", "section"),
        P("section", "ep", None),
        P("section", "ep", None),
        P("section", "ep", None),
    )
    return jax.shard_map(
        on_device,
        mesh=mesh,
        in_specs=placed,
        out_specs=(
            P("section", "ep", None),
            P("section", "ep", None),
            P("section", "ep", None),
            P("section", "ep", None),
        ),
        check_vma=False,
    )
```

time: 51.1 us -> 44.6 us (0.87)
  Pallas kernels: 50.2 us -> 43.8 us
    pallas_call x1, Pallas kernels: 7.99 us -> 3.39 us  [outputs(): pl.pallas_call(outputs_kernel, out_shape=(jax.ShapeDtypeStruct(current.sh...]
    pallas_call x1, Pallas kernels: 42.2 us -> 40.4 us  [exchange(): pl.pallas_call(functools.partial(exchange_kernel, depth), out_shape=(jax....]
where the time goes in v2:
time: 44.6 us; the launch traced here: 44.4 us
  Pallas kernels  43.8 us (98%)
  between operations  0.66 us (1%)
    pallas_call x1, Pallas kernels, exchange(): pl.pallas_call(functools.partial(exchange_kernel, depth), out_shape=(jax....  40.4 us
    pallas_call x1, Pallas kernels, outputs(): pl.pallas_call(outputs_kernel, out_shape=(jax.ShapeDtypeStruct(current.sh...  3.39 us

profile of v2, /device:TPU:0, one launch (start us, length us, event | category | flops | bytes accessed | tf_op | source)
XLA Modules:
  0.0 44.4 jit_solution(2846149079051467291)
XLA Ops:
  0.6 0.0 copy-start
  0.6 40.4 %exchange.1 = (f32[2,2,4,1024]{3,2,1,0:T(4,128)S(1)}, f32[4,128]{1,0:T(4,128)S(1)}, bf16[224,4096]{1,0:T(8,128)(2,1)S(1)}, bf16[224,4096]{1,0:T(8,128)(2,1)S(1)}, bf16[224,4096]{1,0:T(8,128)(2,1)S(1)}) custom-call(s32[2,128]{1,0:T(2,128)} %bitcast.18, f32[2,128]{1,0:T(2,128)} %bitcast.19, bf16[128,4096]{1,0:T(8,128)(2,1)} %bitcast.17, ...), custom_call_target="tpu_custom_call" | custom-call | tf_op jit(solution)/shard_map/exchange/pallas_call | solution.py:309
  41.0 0.0 copy-done
  41.0 3.4 %outputs.1 = (bf16[128,4096]{1,0:T(8,128)(2,1)}, bf16[224,4096]{1,0:T(8,128)(2,1)}, bf16[224,4096]{1,0:T(8,128)(2,1)}, bf16[224,4096]{1,0:T(8,128)(2,1)}) custom-call(f32[2,2,4,1024]{3,2,1,0:T(4,128)S(1)} %get-tuple-element.13.back_ref, f32[4,128]{1,0:T(4,128)S(1)} %get-tuple-element.14.select_ref, bf16[224,4096]{1,0:T(8,128)(2,1)S(1)} %get-tuple-element.15.gate_ref, ...), custom_call_target="tpu_custom_call" | custom-call | tf_op jit(solution)/shard_map/outputs/pallas_call | solution.py:386
Async XLA Ops:
  0.6 40.4 %copy-start = (bf16[128,4096]{1,0:T(8,128)(2,1)S(1)}, bf16[128,4096]{1,0:T(8,128)(2,1)}, u32[]{:S(2)}) copy-start(bf16[128,4096]{1,0:T(8,128)(2,1)} %current_hbm.3) | copy-start | bytes 3145732
